TPU v7x, 128 devices: a whole 4x4x4 slice. The times are simulated.
128 devices in a mesh: cuts: 4 (over x_hi, core), dom: 16 (over y, z), vec: 2 (over x_lo).
Axes of the slice: x: 4 (x_hi: 2, x_lo: 2; x = x_hi * 2 + x_lo), y: 4, z: 4, core: 2. Of those that a mesh axis runs over, the one named last changes fastest.
Arguments:
- starts_old: bfloat16 [4, 2, 32, 1536, 768], P('cuts', None, 'vec', 'dom'), may hold values from -6 to 6
- y_operator: bfloat16 [768, 768], replicated, may hold values from -0.21875 to 0.21875
- coarse_inverse: bfloat16 [1536, 1536], P('vec'), may hold values from -1 to 2
- base_speed: float32 [1536, 768], P('dom'), may hold values from 0.5 to 1.5
- damping: float32 [32], P('vec'), may hold values from 0.5 to 3
- coupling: float32 [32], P('vec'), may hold values from 0.3 to 1.5
Outputs:
- ends_new: float32 [4, 2, 32, 1536, 768], P('cuts', None, 'vec', 'dom')
All inputs are finite; a program needn't handle non-finite values.
Results may differ from a plain program's by a relative error of at most 0.0078.
Values may be sent and summed in bfloat16 or wider, within the bound.
A program may use at most 192 MiB of HBM per device.

v0:
```python
import jax
import jax.numpy as jnp
import numpy as np
from jax import lax
from jax.sharding import PartitionSpec as P

NP = 16


fine_step = 0.25
penalty = 2.0


def from_behind(shard, axis, by):
    size = lax.axis_size(axis)
    pairs = [(i, i + by) for i in range(size) if 0 <= i + by < size]
    return lax.ppermute(shard, axis, pairs)


def in_blocks(shard, dim, size):
    dims = shard.shape
    blocks = shard.reshape(*dims[:dim], size, dims[dim] // size, *dims[dim + 1 :])
    return jnp.moveaxis(blocks, dim, 0)


def cut_rows(length, count):
    hop = length // count
    if hop >= 8:
        hop -= hop % 8
    return [hop * k for k in range(1, count)]


def in_order(blocks, dim):
    blocks = jnp.moveaxis(blocks, 0, dim)
    dims = blocks.shape
    return blocks.reshape(*dims[:dim], dims[dim] * dims[dim + 1], *dims[dim + 2 :])


def exchange_in_pieces(shard, axis, pieces, split_dim, concat_dim):
    blocks = in_blocks(shard, split_dim, lax.axis_size(axis))
    cut = max(range(1, max(2, blocks.ndim - 1)), key=lambda d: blocks.shape[d])
    outs = []
    for section in jnp.split(blocks, cut_rows(blocks.shape[cut], pieces), axis=cut):
        if section.size:
            outs.append(lax.all_to_all(section, axis, split_axis=0, concat_axis=0, tiled=True))
    return in_order(jnp.concatenate(outs, axis=cut), concat_dim)


def cheb_matrix(points_sub):
    indices = np.arange(points_sub)
    points = -np.cos(np.pi * indices / (points_sub - 1))
    edge_weight = np.where((indices == 0) | (indices == points_sub - 1), 2.0, 1.0)
    sign_table = np.where((indices[:, None] + indices[None, :]) % 2 == 0, 1.0, -1.0)
    identity_table = np.eye(points_sub)
    gap_matrix = points[:, None] - points[None, :] + identity_table
    off_diag = (
        edge_weight[:, None]
        / edge_weight[None, :]
        * sign_table
        / gap_matrix
        * (1.0 - identity_table)
    )
    return off_diag - off_diag.sum(axis=1)[:, None] * identity_table


def local(starts_old, y_operator, coarse_inverse, base_speed, damping, coupling):
    start_block = starts_old[0]
    current_state = start_block.astype(jnp.float32)
    part_count, wave_count, column_count, y_count = current_state.shape
    points_sub = NP
    sub_count = column_count // points_sub
    x_scale = 4.0 / (points_sub * points_sub)
    derivative = jnp.asarray(cheb_matrix(points_sub), jnp.float32)
    sign_factor = jnp.array([1.0, -1.0], jnp.float32)[:, None, None, None]
    first_point = (jnp.arange(column_count) % points_sub == 0).astype(jnp.float32)[
        None, None, :, None
    ]
    speed_field = base_speed[None, None]
    full_inverse = lax.all_gather(coarse_inverse, "vec", axis=0, tiled=True)

    def slope_of(values):
        rounded = values.astype(jnp.bfloat16)
        along_y = jnp.dot(
            rounded.reshape(part_count * wave_count * column_count, y_count),
            y_operator,
            preferred_element_type=jnp.float32,
        ).reshape(values.shape)
        blocks = values.reshape(part_count, wave_count, sub_count, points_sub, y_count)
        along_x = jnp.einsum(
            "ij,pwsjy->pwsiy", derivative, blocks, precision=lax.Precision.HIGHEST
        ).reshape(values.shape)
        inflow_row = from_behind(values[:, :, column_count - 1 :, :], "dom", 1)
        previous = jnp.concatenate([inflow_row, values[:, :, : column_count - 1, :]], axis=2)
        jump_term = first_point * (values - previous)
        advect = speed_field * (x_scale * along_x + penalty * jump_term)
        partner = rounded[::-1].astype(jnp.float32)
        return (
            -advect
            + along_y
            + sign_factor * coupling[None, :, None, None] * partner
            - damping[None, :, None, None] * values
        )

    middle = current_state + fine_step * slope_of(current_state)
    fine_end = middle + fine_step * slope_of(middle)
    factor = 1.0 / (1.0 + 2.0 * fine_step * damping)
    is_leader = lax.axis_index("cuts") == 0
    slice_total = lax.axis_size("cuts")
    line_waves = wave_count // lax.axis_size("dom")
    gain = lax.dynamic_slice_in_dim(factor, lax.axis_index("dom") * line_waves, line_waves, 0)[
        None, :, None, None
    ]
    fine_lines = exchange_in_pieces(fine_end.astype(jnp.bfloat16), "dom", 2, 1, 2).astype(
        fine_end.dtype
    )
    start_lines = lax.all_to_all(start_block, "dom", split_axis=1, concat_axis=2, tiled=True)
    line_state = fine_lines
    start_wide = start_lines.astype(jnp.float32)
    for turn_index in range(slice_total - 1):
        arrived = from_behind(line_state.astype(jnp.bfloat16), "cuts", 1)
        gap = (arrived.astype(jnp.float32) - start_wide).astype(jnp.bfloat16)
        mapped = jnp.einsum("ij,pwjy->pwiy", full_inverse, gap, preferred_element_type=jnp.float32)
        line_state = jnp.where(is_leader, fine_lines, fine_lines + gain * mapped)
    block_state = lax.all_to_all(
        line_state.astype(jnp.bfloat16), "dom", split_axis=2, concat_axis=1, tiled=True
    ).astype(line_state.dtype)
    return block_state[None]


def solution(mesh):
    in_specs = (
        P("cuts", None, "vec", "dom", None),
        P(),
        P("vec", None),
        P("dom", None),
        P("vec"),
        P("vec"),
    )
    out_specs = P("cuts", None, "vec", "dom", None)
    return jax.shard_map(local, mesh=mesh, in_specs=in_specs, out_specs=out_specs, check_vma=False)
```

profile of v0, /device:TPU:4, one launch (start us, length us, event | category | flops | bytes accessed | tf_op | source)
XLA Modules:
  0.0 502.2 jit_solution(7625999521766424536)
XLA Ops:
  6.5 0.0 slice-start.1
  6.6 3.6 bitcast_convert_fusion.1
  10.2 0.0 copy-start.2
  10.2 3.7 copy-done.2
  14.0 0.1 slice.16
  14.0 3.8 collective-permute-start
  17.9 0.1 broadcast_multiply_fusion.2
  18.0 6.3 %broadcast_multiply_fusion = f32[16,2,16,6,768]{4,0,3,2,1:T(8,128)} fusion(f32[16,16,1,1,1]{1,0,4,3,2:T(8,128)S(1)} %copy-done.4, bf16[2,16,6,16,768]{4,3,2,1,0:T(8,128)(2,1)S(1)} %bitcast.78), kind=kOutput, calls=%fused_computation.43 | convolution fusion | flops 455344128 | bytes 14156800 | tf_op jit(solution)/shard_map/ij,pwsjy->pwsiy/dot_general | solution.py:89
  24.3 0.0 collective-permute-done
  24.4 16.9 %fusion.37 = (bf16[2,16,96,768]{3,2,1,0:T(8,128)(2,1)}, f32[2,16,96,768]{3,2,1,0:T(8,128)}) fusion(f32[16]{0:T(128)S(1)} %copy-done.8, bf16[2,16,96,768]{3,2,1,0:T(8,128)(2,1)S(1)} %bitcast.79, f32[2,16]{1,0:T(2,128)S(1)} %broadcast_multiply_fusion.2, bf16[768,768]{1,0:T(8,128)(2,1)S(1)} %copy-done, f32[2,16,95,768]{3,2,1,0:T(8,128)} %bitcast.83, ...), kind=kOutput, calls=%fused_computation.54 | convolution fusion | flops 3663986688 | bytes 39223872 | tf_op jit(solution)/shard_map/dot_general | solution.py:83
  41.3 1.2 slice.18
  42.5 4.0 collective-permute-start.1
  46.5 12.9 %broadcast_multiply_fusion.1 = f32[2,16,6,768,16]{3,4,2,1,0:T(8,128)} fusion(f32[2,16,6,16,768]{4,3,2,1,0:T(8,128)} %bitcast.81, f32[16,16,1,1,1]{1,0,4,3,2:T(8,128)S(1)} %copy-done.4), kind=kOutput, calls=%fused_computation.44 | convolution fusion | flops 455344128 | bytes 18875392 | tf_op jit(solution)/shard_map/ij,pwsjy->pwsiy/dot_general | solution.py:89
  59.4 0.0 collective-permute-done.1
  59.4 17.7 %fusion.33 = bf16[16,2,1,96,768]{4,3,0,1,2:T(8,128)(2,1)} fusion(f32[2,16,96,768]{3,2,1,0:T(8,128)} %get-tuple-element.8, f32[16]{0:T(128)S(1)} %copy-done.8, bf16[2,16,96,768]{3,2,1,0:T(8,128)(2,1)} %get-tuple-element.7, f32[2,16]{1,0:T(2,128)S(1)} %broadcast_multiply_fusion.2, f32[2,16,95,768]{3,2,1,0:T(8,128)} %bitcast.82, ...), kind=kOutput, calls=%fused_computation.45 | convolution fusion | flops 3661627392 | bytes 39223872 | tf_op jit(solution)/shard_map/dot_general | solution.py:83
  77.2 4.2 fusion.36
  81.4 1.7 copy.28
  83.1 6.0 %all-to-all-start = ((bf16[16,2,1,48,768]{4,3,1,2,0:T(8,128)(2,1)}), bf16[16,2,1,48,768]{4,3,1,2,0:T(8,128)(2,1)S(1)}, u32[]{:S(2)}, u32[]{:S(2)}) async-start(bf16[16,2,1,48,768]{4,3,1,2,0:T(8,128)(2,1)} %copy.28), calls=%async_computation | async-start | bytes 4718592 | tf_op jit(solution)/shard_map/all_to_all | solution.py:45
  89.1 3.4 copy.29
  92.5 29.3 %all-to-all-done = bf16[16,2,1,48,768]{4,3,1,2,0:T(8,128)(2,1)S(1)} async-done(((bf16[16,2,1,48,768]{4,3,1,2,0:T(8,128)(2,1)}), bf16[16,2,1,48,768]{4,3,1,2,0:T(8,128)(2,1)S(1)}, u32[]{:S(2)}, u32[]{:S(2)}) %all-to-all-start) | async-done | bytes 2359328 | tf_op jit(solution)/shard_map/all_to_all | solution.py:45
  121.8 4.5 all-to-all-start.1
  126.3 4.9 copy.33
  131.2 25.2 %all-to-all-done.1 = bf16[16,2,1,48,768]{4,3,1,2,0:T(8,128)(2,1)} async-done(((bf16[16,2,1,48,768]{4,3,1,2,0:T(8,128)(2,1)}), bf16[16,2,1,48,768]{4,3,1,2,0:T(8,128)(2,1)}, u32[]{:S(2)}, u32[]{:S(2)}) %all-to-all-start.1) | async-done | bytes 2359328 | tf_op jit(solution)/shard_map/all_to_all | solution.py:45
  156.4 4.9 all-to-all-start.2
  161.3 0.0 all-gather.2.cloned.1.call-start
  161.3 0.7 all-gather.2.cloned.1.call-update
  162.0 2.1 pad_maximum_fusion
  164.2 2.5 copy.43
  166.7 2.1 collective-permute-start.2
  168.8 0.6 dynamic_slice.3
  169.4 6.7 %copy.32 = bf16[2,1,1536,768]{2,3,0,1:T(8,128)(2,1)} copy(bf16[2,1,1536,768]{3,2,0,1:T(8,128)(2,1)} %bitcast.17) | data formatting | bytes 9437184 | tf_op jit(solution)/shard_map/reshape | solution.py:36
  176.2 43.4 %all-to-all-done.2 = bf16[2,16,96,768]{3,2,0,1:T(8,128)(2,1)} async-done(((bf16[2,16,96,768]{3,2,0,1:T(8,128)(2,1)}), bf16[2,16,96,768]{3,2,0,1:T(8,128)(2,1)}, u32[]{:S(2)}, u32[]{:S(2)}) %all-to-all-start.2) | async-done | bytes 4718624 | tf_op jit(solution)/shard_map/all_to_all | solution.py:116
  219.6 2.7 copy.34
  222.3 4.8 bitcast_convert_fusion
  227.0 3.0 all-gather.2.cloned.1.call-done
  230.1 44.4 %collective-permute-done.2 = bf16[2,1,1536,768]{3,2,0,1:T(8,128)(2,1)} collective-permute-done((bf16[2,1,1536,768]{3,2,0,1:T(8,128)(2,1)}, bf16[2,1,1536,768]{3,2,0,1:T(8,128)(2,1)}, u32[]{:S(2)}, u32[]{:S(2)}) %collective-permute-start.2) | collective-permute-done | bytes 4718624 | tf_op jit(solution)/shard_map/ppermute | solution.py:17
  274.5 17.4 %fusion = bf16[2,1,1536,768]{2,3,0,1:T(8,128)(2,1)} fusion(bf16[2,1,1536,768]{2,3,0,1:T(8,128)(2,1)} %copy.32, f32[2,1,1536,768]{3,2,0,1:T(8,128)} %bitcast_convert_fusion, bf16[2,1,1536,768]{3,2,0,1:T(8,128)(2,1)} %collective-permute-done.2, bf16[1536,1536]{1,0:T(8,128)(2,1)} %all-gather.2.cloned.1.call-done, f32[]{:T(128)} %bitcast.18, pred[]{:T(512)S(6)} %eq.15), kind=kOutput, calls=%fused_computation.6 | convolution fusion | flops 7266631680 | bytes 28311556 | tf_op jit(solution)/shard_map/ij,pwjy->pwiy/dot_general | solution.py:122
  291.9 1.9 collective-permute-start.3
  293.8 9.7 %copy.36 = f32[2,1,1536,768]{2,3,0,1:T(8,128)} copy(f32[2,1,1536,768]{3,2,0,1:T(8,128)} %bitcast_convert_fusion) | data formatting | bytes 18874368 | tf_op jit(solution)/shard_map/convert_element_type | solution.py:118
  303.5 45.7 %collective-permute-done.3 = bf16[2,1,1536,768]{2,3,0,1:T(8,128)(2,1)} collective-permute-done((bf16[2,1,1536,768]{2,3,0,1:T(8,128)(2,1)}, bf16[2,1,1536,768]{2,3,0,1:T(8,128)(2,1)}, u32[]{:S(2)}, u32[]{:S(2)}) %collective-permute-start.3) | collective-permute-done | bytes 4718624 | tf_op jit(solution)/shard_map/ppermute | solution.py:17
  349.1 17.0 %fusion.1 = bf16[2,1,1536,768]{2,3,0,1:T(8,128)(2,1)} fusion(bf16[2,1,1536,768]{2,3,0,1:T(8,128)(2,1)} %copy.32, f32[2,1,1536,768]{2,3,0,1:T(8,128)} %copy.36, bf16[2,1,1536,768]{2,3,0,1:T(8,128)(2,1)} %collective-permute-done.3, bf16[1536,1536]{1,0:T(8,128)(2,1)} %all-gather.2.cloned.1.call-done, f32[]{:T(128)} %bitcast.18, pred[]{:T(512)S(6)} %eq.15), kind=kOutput, calls=%fused_computation.7 | convolution fusion | flops 7266631680 | bytes 28311556 | tf_op jit(solution)/shard_map/ij,pwjy->pwiy/dot_general | solution.py:122
  366.1 2.2 collective-permute-start.4
  368.3 55.1 %collective-permute-done.4 = bf16[2,1,1536,768]{2,3,0,1:T(8,128)(2,1)} collective-permute-done((bf16[2,1,1536,768]{2,3,0,1:T(8,128)(2,1)}, bf16[2,1,1536,768]{2,3,0,1:T(8,128)(2,1)}, u32[]{:S(2)}, u32[]{:S(2)}) %collective-permute-start.4) | collective-permute-done | bytes 4718624 | tf_op jit(solution)/shard_map/ppermute | solution.py:17
  423.3 14.3 %fusion.2 = bf16[2,1,1536,768]{2,3,0,1:T(8,128)(2,1)} fusion(bf16[2,1,1536,768]{2,3,0,1:T(8,128)(2,1)} %copy.32, f32[2,1,1536,768]{2,3,0,1:T(8,128)S(1)} %copy-done.3, bf16[2,1,1536,768]{2,3,0,1:T(8,128)(2,1)} %collective-permute-done.4, bf16[1536,1536]{1,0:T(8,128)(2,1)} %all-gather.2.cloned.1.call-done, f32[]{:T(128)} %bitcast.18, pred[]{:T(512)S(6)} %eq.15), kind=kOutput, calls=%fused_computation.8 | convolution fusion | flops 7266631680 | bytes 28311556 | tf_op jit(solution)/shard_map/ij,pwjy->pwiy/dot_general | solution.py:122
  437.6 12.5 %copy.38 = bf16[2,1,1536,768]{3,0,1,2:T(2,128)(2,1)} copy(bf16[2,1,1536,768]{2,3,0,1:T(8,128)(2,1)} %fusion.2) | data formatting | bytes 9437184 | tf_op jit(solution)/shard_map/convert_element_type | solution.py:125
  450.1 39.7 %all_to_all.28 = bf16[2,1,1536,768]{3,0,1,2:T(2,128)(2,1)S(1)} all-to-all(bf16[2,1,1536,768]{3,0,1,2:T(2,128)(2,1)} %copy.38), channel_id=1, replica_groups=mesh['cuts'=4,'dom'=16,'vec'=2] {'dom'}, dimensions={2} | all-to-all | bytes 9437184 | tf_op jit(solution)/shard_map/all_to_all | solution.py:124
  489.8 0.6 copy.39
  490.4 4.9 convert.3
  (22 shorter events, 0.0 us)
Async XLA Ops:
  6.5 17.8 %copy-start = (bf16[768,768]{1,0:T(8,128)(2,1)S(1)}, bf16[768,768]{1,0:T(8,128)(2,1)}, u32[]{:S(2)}) copy-start(bf16[768,768]{1,0:T(8,128)(2,1)} %param.9) | copy-start | bytes 3538948
  6.5 11.3 %copy-start.6 = (f32[2]{0:T(128)S(1)}, f32[2]{0:T(128)}, u32[]{:S(2)}) copy-start(f32[2]{0:T(128)} %constant.45.clone) | copy-start | bytes 28
  6.5 11.4 %copy-start.4 = (f32[16,16,1,1,1]{1,0,4,3,2:T(8,128)S(1)}, f32[16,16,1,1,1]{1,0,4,3,2:T(8,128)}, u32[]{:S(2)}) copy-start(f32[16,16,1,1,1]{1,0,4,3,2:T(8,128)} %constant.47) | copy-start | bytes 3076
  6.5 11.4 %slice-start = ((s8[4718592]{0:T(1024)(128)(4,1)}), s8[524288]{0:T(1024)(128)(4,1)S(1)}, s32[]{:S(2)}) async-start(s8[4718592]{0:T(1024)(128)(4,1)} %bitcast.76), calls=%async_computation.5 | async-start | bytes 1048576
  6.5 11.4 %copy-start.5 = (f32[16]{0:T(128)S(1)}, f32[16]{0:T(128)}, u32[]{:S(2)}) copy-start(f32[16]{0:T(128)} %param.13) | copy-start | bytes 196
  6.5 11.4 %slice-start.1 = ((s8[4718592]{0:T(1024)(128)(4,1)}), s8[4194304]{0:T(1024)(128)(4,1)S(1)}, s32[]{:S(2)}) async-start(s8[4718592]{0:T(1024)(128)(4,1)} %bitcast.76), calls=%async_computation.6 | async-start | bytes 8388608
  10.2 3.7 copy-start.2
  14.0 10.4 %copy-start.7 = (f32[96,768]{1,0:T(8,128)S(1)}, f32[96,768]{1,0:T(8,128)}, u32[]{:S(2)}) copy-start(f32[96,768]{1,0:T(8,128)} %param.11) | copy-start | bytes 884740
  14.0 10.4 %copy-start.8 = (f32[16]{0:T(128)S(1)}, f32[16]{0:T(128)}, u32[]{:S(2)}) copy-start(f32[16]{0:T(128)} %param.12) | copy-start | bytes 196
  14.0 10.3 %collective-permute-start = (f32[2,16,1,768]{3,2,1,0:T(1,128)S(1)}, f32[2,16,1,768]{3,2,1,0:T(1,128)S(1)}, u32[]{:S(2)}, u32[]{:S(2)}) collective-permute-start(f32[2,16,1,768]{3,2,1,0:T(1,128)S(1)} %slice.16), channel_id=1, source_target_pairs={{0,2},{2,4},{4,6},{6,8},{8,10},{10,12},{12,14},{14,16},{16,18},{18... | collective-permute-start | bytes 294920 | tf_op jit(solution)/shard_map/ppermute | solution.py:17
  42.5 16.9 %collective-permute-start.1 = (f32[2,16,1,768]{3,2,1,0:T(1,128)S(1)}, f32[2,16,1,768]{3,2,1,0:T(1,128)S(1)}, u32[]{:S(2)}, u32[]{:S(2)}) collective-permute-start(f32[2,16,1,768]{3,2,1,0:T(1,128)S(1)} %slice.18), channel_id=1, source_target_pairs={{0,2},{2,4},{4,6},{6,8},{8,10},{10,12},{12,14},{14,16},{16,18},{18... | collective-permute-start | bytes 294920 | tf_op jit(solution)/shard_map/ppermute | solution.py:17
  83.1 38.7 %all-to-all-start = ((bf16[16,2,1,48,768]{4,3,1,2,0:T(8,128)(2,1)}), bf16[16,2,1,48,768]{4,3,1,2,0:T(8,128)(2,1)S(1)}, u32[]{:S(2)}, u32[]{:S(2)}) async-start(bf16[16,2,1,48,768]{4,3,1,2,0:T(8,128)(2,1)} %copy.28), calls=%async_computation | async-start | bytes 4718592 | tf_op jit(solution)/shard_map/all_to_all | solution.py:45
  121.8 34.6 %all-to-all-start.1 = ((bf16[16,2,1,48,768]{4,3,1,2,0:T(8,128)(2,1)}), bf16[16,2,1,48,768]{4,3,1,2,0:T(8,128)(2,1)}, u32[]{:S(2)}, u32[]{:S(2)}) async-start(bf16[16,2,1,48,768]{4,3,1,2,0:T(8,128)(2,1)} %copy.29), calls=%async_computation.1 | async-start | bytes 4718592 | tf_op jit(solution)/shard_map/all_to_all | solution.py:45
  156.4 63.2 %all-to-all-start.2 = ((bf16[2,16,96,768]{3,2,0,1:T(8,128)(2,1)}), bf16[2,16,96,768]{3,2,0,1:T(8,128)(2,1)}, u32[]{:S(2)}, u32[]{:S(2)}) async-start(bf16[2,16,96,768]{3,2,0,1:T(8,128)(2,1)} %copy.33), calls=%async_computation.2 | async-start | bytes 9437184 | tf_op jit(solution)/shard_map/all_to_all | solution.py:116
  161.3 68.8 %all-gather.2.cloned.1.call-start = ((), (), s32[]{:S(2)}) async-start(), calls=%async_computation.4 | async-start | bytes 7077888 | tf_op jit(solution)/shard_map/all_gather | solution.py:79
  166.7 107.8 %collective-permute-start.2 = (bf16[2,1,1536,768]{3,2,0,1:T(8,128)(2,1)}, bf16[2,1,1536,768]{3,2,0,1:T(8,128)(2,1)}, u32[]{:S(2)}, u32[]{:S(2)}) collective-permute-start(bf16[2,1,1536,768]{3,2,0,1:T(8,128)(2,1)} %bitcast.17), channel_id=1, source_target_pairs={{0,32},{32,64},{64,96},{1,33},{33,65},{65,97},{2,34},{34,66},{66,9... | collective-permute-start | bytes 14155784 | tf_op jit(solution)/shard_map/ppermute | solution.py:17
  291.9 57.3 %collective-permute-start.3 = (bf16[2,1,1536,768]{2,3,0,1:T(8,128)(2,1)}, bf16[2,1,1536,768]{2,3,0,1:T(8,128)(2,1)}, u32[]{:S(2)}, u32[]{:S(2)}) collective-permute-start(bf16[2,1,1536,768]{2,3,0,1:T(8,128)(2,1)} %fusion), channel_id=1, source_target_pairs={{0,32},{32,64},{64,96},{1,33},{33,65},{65,97},{2,34},{34,66},{66,9... | collective-permute-start | bytes 14155784 | tf_op jit(solution)/shard_map/ppermute | solution.py:17
  303.5 119.9 %copy-start.3 = (f32[2,1,1536,768]{2,3,0,1:T(8,128)S(1)}, f32[2,1,1536,768]{2,3,0,1:T(8,128)}, u32[]{:S(2)}) copy-start(f32[2,1,1536,768]{2,3,0,1:T(8,128)} %copy.36) | copy-start | bytes 28311556
  366.1 57.3 %collective-permute-start.4 = (bf16[2,1,1536,768]{2,3,0,1:T(8,128)(2,1)}, bf16[2,1,1536,768]{2,3,0,1:T(8,128)(2,1)}, u32[]{:S(2)}, u32[]{:S(2)}) collective-permute-start(bf16[2,1,1536,768]{2,3,0,1:T(8,128)(2,1)} %fusion.1), channel_id=1, source_target_pairs={{0,32},{32,64},{64,96},{1,33},{33,65},{65,97},{2,34},{34,66},{66,9... | collective-permute-start | bytes 14155784 | tf_op jit(solution)/shard_map/ppermute | solution.py:17
  489.8 5.5 %copy-start.1 = (bf16[768,768]{1,0:T(8,128)(2,1)S(1)}, bf16[768,768]{1,0:T(8,128)(2,1)}, u32[]{:S(2)}) copy-start(bf16[768,768]{1,0:T(8,128)(2,1)} %param.9) | copy-start | bytes 3538948
Sparse Core Ops, SparseCore 0:
  163.7 66.2 all-gather.1
where the time goes:
time: 503 us; the launch traced here: 502 us
  waiting for transfers between devices  247 us (49%)
  matrix products  103 us (20%)
  local copies, waits for them, and re-layouts  54.5 us (11%)
  blocking collectives  39.7 us (8%)
  starting transfers between devices  29.5 us (6%)
  other arithmetic  15.5 us (3%)
  between operations  13.6 us (3%)
    ppermute x5, waiting for transfers between devices, from_behind(): return lax.ppermute(shard, axis, pairs)  145 us
    all_to_all x2, waiting for transfers between devices, exchange_in_pieces(): lax.all_to_all(section, axis, split_axis=0, concat_axis=0, tiled=True)  54.5 us
    dot_general x3, matrix products, local(): jnp.einsum('ij,pwjy->pwiy', full_inverse, gap, preferred_element_type=jnp...  48.6 us
    all_to_all x1, waiting for transfers between devices, local(): lax.all_to_all(start_block, 'dom', split_axis=1, concat_axis=2, tiled=True)  43.4 us
    all_to_all x1, blocking collectives, local(): lax.all_to_all(line_state.astype(jnp.bfloat16), 'dom', split_axis=2, conc...  39.7 us
    dot_general x2, matrix products, slope_of(): jnp.dot(rounded.reshape(part_count * wave_count * column_count, y_count),...  34.7 us
    dot_general x2, matrix products, slope_of(): jnp.einsum('ij,pwsjy->pwsiy', derivative, blocks, precision=lax.Precision...  19.3 us
    ppermute x5, starting transfers between devices, from_behind(): return lax.ppermute(shard, axis, pairs)  14 us
  transfers between devices with their start and end apart: 9, of which 7 were waited for; matrix products, arithmetic and copies ran while one was open for 11% of the time, Pallas kernels for 0%

commit v1 on v0

v1 whole, which is shorter than its diff:
```python
import functools

import jax
import jax.numpy as jnp
import numpy as np
from jax import lax
from jax.experimental import pallas as pl
from jax.experimental.pallas import tpu as pltpu
from jax.sharding import PartitionSpec as P

NP = 16
MESH = pl.DeviceIdType.MESH
F32 = jnp.float32
BF16 = jnp.bfloat16

fine_step = 0.25
penalty = 2.0
lanes = 256
pair = 2


def cheb_matrix(points_sub):
    indices = np.arange(points_sub)
    points = -np.cos(np.pi * indices / (points_sub - 1))
    edge_weight = np.where((indices == 0) | (indices == points_sub - 1), 2.0, 1.0)
    sign_table = np.where((indices[:, None] + indices[None, :]) % 2 == 0, 1.0, -1.0)
    identity_table = np.eye(points_sub)
    gap_matrix = points[:, None] - points[None, :] + identity_table
    off_diag = (
        edge_weight[:, None]
        / edge_weight[None, :]
        * sign_table
        / gap_matrix
        * (1.0 - identity_table)
    )
    return off_diag - off_diag.sum(axis=1)[:, None] * identity_table


def advect_matrix(columns):
    derivative = cheb_matrix(NP).astype(np.float32).astype(np.float64)
    table = np.kron(np.eye(columns // NP), derivative) * (4.0 / (NP * NP))
    for row in range(0, columns, NP):
        table[row, row] += penalty
        if row:
            table[row, row - 1] -= penalty
    return fine_step * table


def kernel(
    ny, nz, s_hbm, y_hbm, g_hbm, speed_hbm, a_ref, tail_ref, damp_ref, coup_ref,
    f_hbm, c_hbm,
    s_own, s_next, tails, yop, speed, fine, mid, midb, ax, ay, halo_f, halo_b, halo_in, inflow,
    dsend, lines, cbuf, gmat,
    in_sem, misc_sem, next_send, next_recv, g_send, g_recv, g_local, halo_send, halo_recv,
    line_send, line_recv, x_send, c_send, c_recv, c_local, f_sem,
):
    k = lax.axis_index("cuts")
    j = lax.axis_index("dom")
    v = lax.axis_index("vec")
    y, z = j // nz, lax.rem(j, nz)
    core = lax.rem(k, 2)
    low = k < 2
    dom = ny * nz
    _, waves, cols, ysize = s_hbm.shape
    chunks = ysize // lanes
    half = g_hbm.shape[0]
    quarter = half // 4

    def order(t):
        ty = lax.rem(t, ny)
        tz = lax.rem(t // ny + (nz - 1) * ty, nz)
        return lax.rem(y + ty, ny) * nz + lax.rem(z + tz, nz)

    def remote(src, dst, send, recv, at):
        return pltpu.make_async_remote_copy(
            src_ref=src, dst_ref=dst, send_sem=send, recv_sem=recv, device_id=at, device_id_type=MESH
        )

    load_tails = pltpu.make_async_copy(s_hbm.at[:, :, pl.ds(cols - NP, NP), :], tails, misc_sem.at[0])
    load_y = pltpu.make_async_copy(y_hbm, yop, misc_sem.at[1])
    load_speed = pltpu.make_async_copy(speed_hbm, speed, misc_sem.at[2])
    load_tails.start()
    load_y.start()
    load_speed.start()

    def load_wave(w):
        return pltpu.make_async_copy(s_hbm.at[:, w], s_own.at[w], in_sem.at[w])

    def start_wave(t, carry):
        load_wave(order(t)).start()
        return carry

    lax.fori_loop(0, waves, start_wave, 0)

    own_at = pl.multiple_of(v * half, half)
    other_at = pl.multiple_of((1 - v) * half, half)
    load_g = pltpu.make_async_copy(g_hbm, gmat.at[pl.ds(own_at, half)], g_local)
    load_g.start()

    def send_g(side):
        rows = pl.multiple_of((2 * side + core) * quarter, quarter)
        at = (k if side == 0 else lax.rem(k + 2, 4), j, 1 - v)
        return remote(
            g_hbm.at[pl.ds(rows, quarter)],
            gmat.at[pl.ds(pl.multiple_of(own_at + rows, quarter), quarter)],
            g_send.at[side], g_recv.at[side], at,
        )

    def pass_g(side):
        rows = pl.multiple_of(other_at + (2 * side + core) * quarter, quarter)
        part = gmat.at[pl.ds(rows, quarter)]
        return remote(part, part, g_send.at[2 + side], g_recv.at[2 + side], (k + 1 - 2 * core, j, v))

    send_g(0).start()
    send_g(1).start()

    def send_next(i, w, at):
        return remote(
            s_hbm.at[:, w, :, pl.ds(i * lanes, lanes)], s_next.at[i, w], next_send, next_recv.at[i, w], at
        )

    @pl.when(k > 0)
    def _():
        for i in range(chunks):

            def start_next(t, carry):
                send_next(i, order(t), (k - 1, j, v)).start()
                return carry

            lax.fori_loop(0, waves, start_next, 0)

    load_tails.wait()
    load_y.wait()
    load_speed.wait()
    yop[...] = (yop[...].astype(F32) * fine_step).astype(BF16)

    def gather_tail(w, carry):
        for p in range(2):
            rows = tails[p, w].astype(F32)
            at = pl.ds(p * waves + w, 1)
            halo_f[0, at, :] = rows[NP - 1 : NP, :]
            halo_f[1, at, :] = jnp.sum(rows * tail_ref[:, 0:1], axis=0, keepdims=True)
        return carry

    lax.fori_loop(0, waves, gather_tail, 0)
    halo_b[0] = halo_f[0].astype(BF16)
    halo_f[2] = jnp.dot(halo_b[0], yop[...], preferred_element_type=F32)

    def middle_tail(w, carry):
        keep = 1.0 - fine_step * damp_ref[w]
        cross = fine_step * coup_ref[w]
        for p in range(2):
            at = pl.ds(p * waves + w, 1)
            other = pl.ds((1 - p) * waves + w, 1)
            swap = cross if p == 0 else -cross
            halo_f[3, at, :] = (
                keep * halo_f[0, at, :]
                + halo_f[2, at, :]
                + swap * halo_f[0, other, :]
                - speed[cols - 1 : cols, :] * halo_f[1, at, :]
            )
        return carry

    lax.fori_loop(0, waves, middle_tail, 0)
    halo_b[1] = halo_f[3].astype(BF16)

    def send_halo():
        return remote(halo_b, halo_in, halo_send, halo_recv, (k, j + 1, v))

    @pl.when(j < dom - 1)
    def _():
        send_halo().start()

    @pl.when(j > 0)
    def _():
        remote(halo_b, halo_in, halo_send, halo_recv, (k, j - 1, v)).wait_recv()
        inflow[...] = (fine_step * penalty) * halo_in[...].astype(F32)

    @pl.when(j == 0)
    def _():
        inflow[...] = jnp.zeros_like(inflow)

    first = lax.broadcasted_iota(jnp.int32, (NP, ysize), 0) == 0

    def slope_products(values):
        flat = jnp.concatenate([x.reshape(2 * cols, ysize) for x in values], axis=0)
        for at in range(0, ysize, lanes):
            ay[:, at : at + lanes] = jnp.dot(flat, yop[:, at : at + lanes], preferred_element_type=F32)
        for q, x in enumerate(values):
            for p in range(2):
                ax[q, p] = jnp.dot(a_ref[...], x[p], preferred_element_type=F32)

    def combine(q, w, stage, own, partner, put):
        keep = 1.0 - fine_step * damp_ref[w]
        cross = fine_step * coup_ref[w]
        for p in range(2):
            swap = cross if p == 0 else -cross
            for r in range(0, cols, NP):
                along_x = ax[q, p, r : r + NP, :]
                if r == 0:
                    row = inflow[stage, pl.ds(p * waves + w, 1), :]
                    along_x = along_x - jnp.where(first, row, 0.0)
                at = (2 * q + p) * cols + r
                put(
                    p,
                    r,
                    keep * own(p, r)
                    + ay[at : at + NP, :]
                    + swap * partner(1 - p, r)
                    - speed[r : r + NP, :] * along_x,
                )

    def emit(i, w):
        @pl.when(k < 3)
        def _():
            send_next(i, w, (k + 1, j, v)).wait_recv()
            for p in range(2):
                gap = (fine[w, p, :, i * lanes : (i + 1) * lanes] - s_next[i, w, p].astype(F32)).astype(BF16)
                target = lines.at[core, i, pl.ds(pl.multiple_of(j * cols, cols), cols)]
                mine = (w == j) & (core == p)

                @pl.when(mine)
                def _():
                    target[...] = gap

                @pl.when(jnp.logical_not(mine))
                def _():
                    dsend[i, w, p] = gap
                    remote(
                        dsend.at[i, w, p], target, line_send.at[p], line_recv.at[core, i],
                        (k - core + p, w, v),
                    ).start()

    def store_fine(w):
        return pltpu.make_async_copy(fine.at[w], f_hbm.at[:, w], f_sem)

    def fine_waves(t, carry):
        ws = [order(t * pair + q) for q in range(pair)]
        for w in ws:
            load_wave(w).wait()
        slope_products([s_own[w] for w in ws])
        for q, w in enumerate(ws):

            def put_middle(p, r, value):
                mid[q, p, r : r + NP, :] = value
                midb[q, p, r : r + NP, :] = value.astype(BF16)

            def start_rows(p, r):
                return s_own[w, p, r : r + NP, :].astype(F32)

            combine(q, w, 0, start_rows, start_rows, put_middle)
        slope_products([midb[q] for q in range(pair)])
        for q, w in enumerate(ws):

            def put_fine(p, r, value):
                fine[w, p, r : r + NP, :] = value

            combine(
                q, w, 1,
                lambda p, r: mid[q, p, r : r + NP, :],
                lambda p, r: midb[q, p, r : r + NP, :].astype(F32),
                put_fine,
            )
            store_fine(w).start()

            @pl.when(k != 1)
            def _():
                emit(0, w)

        return carry

    lax.fori_loop(0, waves // pair, fine_waves, 0)

    def emit_chunk(i):
        def step(t, carry):
            emit(i, order(t))
            return carry

        lax.fori_loop(0, waves, step, 0)

    @pl.when(k == 1)
    def _():
        emit_chunk(0)

    for side in range(2):
        send_g(side).wait_recv()
        pass_g(side).start()
    for i in range(1, chunks):
        emit_chunk(i)
    load_g.wait()
    for side in range(2):
        pass_g(side).wait_recv()

    gain = 1.0 / (1.0 + 2.0 * fine_step * jnp.full((1, lanes), damp_ref[j], F32))
    group = nz * cols

    def wait_lines(b, i, less):
        part = lines.at[b, i, pl.ds(0, (dom - less) * cols)]
        remote(part, part, line_send.at[b], line_recv.at[b, i], (k, j, v)).wait_recv()

    def piece_of(source, i, at, to, queue):
        rows = pl.ds(pl.multiple_of(at * cols, cols), cols)
        spot = c_hbm.at[core, j, :, pl.ds(i * lanes, lanes)]
        return remote(source.at[rows], spot, c_send.at[queue], c_recv.at[core, i], (to, at, v))

    def own_piece(source, i, at):
        rows = pl.ds(pl.multiple_of(at * cols, cols), cols)
        return pltpu.make_async_copy(source.at[rows], c_hbm.at[core, j, :, pl.ds(i * lanes, lanes)], c_local.at[i])

    def send_pieces(source, i, block, to, queue):
        def step(t, carry):
            at = block * nz + lax.rem(z + t, nz)
            mine = (at == j) & (k == to)

            @pl.when(mine)
            def _():
                own_piece(source, i, at).start()

            @pl.when(jnp.logical_not(mine))
            def _():
                piece_of(source, i, at, to, queue).start()

            return carry

        lax.fori_loop(0, nz, step, 0)

    def product(source, out, after):
        def step(t, carry):
            block = lax.rem(y + t, ny)
            rows = pl.ds(pl.multiple_of(block * group, group), group)
            total = jnp.dot(gmat[rows, :], source[...], preferred_element_type=F32)
            out[rows, :] = (gain * total).astype(BF16)
            after(block, rows)
            return carry

        lax.fori_loop(0, ny, step, 0)

    def add_lines(target, term):
        def step(t, carry):
            rows = pl.ds(pl.multiple_of(t * cols, cols), cols)
            target[rows, :] = (target[rows, :].astype(F32) + term[rows, :].astype(F32)).astype(BF16)
            return carry

        lax.fori_loop(0, dom, step, 0)

    def across(i, rows):
        return remote(cbuf.at[1, i, rows], lines.at[1, i, rows], x_send, line_recv.at[1, i], (k + 2, j, v))

    for i in range(chunks):

        @pl.when(core == 0)
        def _():
            wait_lines(0, i, 1)

        @pl.when(core == 1)
        def _():
            wait_lines(0, i, 0)

        @pl.when(low)
        def _():
            product(lines.at[0, i], cbuf.at[0, i], lambda block, rows: send_pieces(cbuf.at[0, i], i, block, 1, 0))

            @pl.when(core == 0)
            def _():
                wait_lines(1, i, 0)

            @pl.when(core == 1)
            def _():
                wait_lines(1, i, 1)

            add_lines(lines.at[1, i], cbuf.at[0, i])
            product(lines.at[1, i], cbuf.at[1, i], lambda block, rows: across(i, rows).start())

        @pl.when(jnp.logical_not(low))
        def _():
            wait_lines(1, i, 0)

            def forward(t, carry):
                send_pieces(lines.at[1, i], i, lax.rem(y + t, ny), 2, 1)
                return carry

            lax.fori_loop(0, ny, forward, 0)
            add_lines(lines.at[0, i], lines.at[1, i])
            product(lines.at[0, i], cbuf.at[0, i], lambda block, rows: send_pieces(cbuf.at[0, i], i, block, 3, 0))

    def done(part, send, recv):
        return remote(part, part, send, recv, (k, j, v))

    def block_of(less):
        return cbuf.at[0, :, pl.ds(0, (dom - less) * cols)]

    def line_of(less):
        return cbuf.at[0, 0, pl.ds(0, (dom - less) * cols)]

    for p in range(2):

        @pl.when(core == p)
        def _():
            @pl.when(k > 0)
            def _():
                for i in range(chunks):
                    done(line_of(1), c_send.at[0], c_recv.at[p, i]).wait_recv()
                    done(line_of(0), c_send.at[0], c_recv.at[1 - p, i]).wait_recv()
                    own_piece(cbuf.at[0, i], i, 0).wait()

            @pl.when(k < 3)
            def _():
                done(block_of(1), line_send.at[p], c_recv.at[0, 0]).wait_send()
                done(block_of(0), line_send.at[1 - p], c_recv.at[0, 0]).wait_send()

            done(block_of(p), c_send.at[0], c_recv.at[0, 0]).wait_send()

            @pl.when(jnp.logical_not(low))
            def _():
                done(block_of(1 - p), c_send.at[1], c_recv.at[0, 0]).wait_send()

    @pl.when(k > 0)
    def _():
        done(s_next, next_send, next_recv.at[0, 0]).wait_send()

    @pl.when(low)
    def _():
        done(block_of(0), x_send, c_recv.at[0, 0]).wait_send()

    @pl.when(j < dom - 1)
    def _():
        send_halo().wait_send()

    for side in range(2):
        send_g(side).wait_send()
        pass_g(side).wait_send()
    pltpu.make_async_copy(f_hbm, f_hbm, f_sem).wait()


def call(torus, state, y_operator, coarse_inverse, base_speed, damping, coupling):
    ny, nz = torus
    dom = ny * nz
    parts, waves, cols, ysize = state.shape
    assert parts == 2 and waves == dom and ysize % lanes == 0 and waves % pair == 0
    chunks = ysize // lanes
    length = dom * cols
    table = advect_matrix(cols)
    a_mat = jnp.asarray(table, BF16)
    tail = jnp.broadcast_to(jnp.asarray(table[-1, -NP:], F32)[:, None], (NP, 128))
    anywhere = pl.BlockSpec(memory_space=pl.ANY)
    vmem = pl.BlockSpec(memory_space=pltpu.VMEM)
    smem = pl.BlockSpec(memory_space=pltpu.SMEM)
    dma = pltpu.SemaphoreType.DMA
    return pl.pallas_call(
        functools.partial(kernel, ny, nz),
        out_shape=(
            jax.ShapeDtypeStruct(state.shape, F32),
            jax.ShapeDtypeStruct(state.shape, BF16),
        ),
        in_specs=[anywhere] * 4 + [vmem] * 2 + [smem] * 2,
        out_specs=(anywhere, anywhere),
        scratch_shapes=[
            pltpu.VMEM((waves, 2, cols, ysize), BF16),
            pltpu.VMEM((chunks, waves, 2, cols, lanes), BF16),
            pltpu.VMEM((2, waves, NP, ysize), BF16),
            pltpu.VMEM((ysize, ysize), BF16),
            pltpu.VMEM((cols, ysize), F32),
            pltpu.VMEM((waves, 2, cols, ysize), F32),
            pltpu.VMEM((pair, 2, cols, ysize), F32),
            pltpu.VMEM((pair, 2, cols, ysize), BF16),
            pltpu.VMEM((pair, 2, cols, ysize), F32),
            pltpu.VMEM((pair * 2 * cols, ysize), F32),
            pltpu.VMEM((4, 2 * waves, ysize), F32),
            pltpu.VMEM((2, 2 * waves, ysize), BF16),
            pltpu.VMEM((2, 2 * waves, ysize), BF16),
            pltpu.VMEM((2, 2 * waves, ysize), F32),
            pltpu.VMEM((chunks, waves, 2, cols, lanes), BF16),
            pltpu.VMEM((2, chunks, length, lanes), BF16),
            pltpu.VMEM((2, chunks, length, lanes), BF16),
            pltpu.VMEM((length, length), BF16),
            dma((waves,)),
            dma((3,)),
            dma,
            dma((chunks, waves)),
            dma((4,)),
            dma((4,)),
            dma,
            dma,
            dma,
            dma((2,)),
            dma((2, chunks)),
            dma,
            dma((2,)),
            dma((2, chunks)),
            dma((chunks,)),
            dma,
        ],
        compiler_params=pltpu.CompilerParams(has_side_effects=True, vmem_limit_bytes=62 * 2**20),
        name="parareal",
    )(state, y_operator, coarse_inverse, base_speed, a_mat, tail, damping, coupling)


def local(torus, starts_old, y_operator, coarse_inverse, base_speed, damping, coupling):
    fine_end, change = call(torus, starts_old[0], y_operator, coarse_inverse, base_speed, damping, coupling)
    is_leader = lax.axis_index("cuts") == 0
    return jnp.where(is_leader, fine_end, fine_end + change.astype(F32))[None]


def solution(mesh):
    dom = mesh.shape["dom"]
    torus = (4, 4) if dom == 16 else (1, dom)
    in_specs = (
        P("cuts", None, "vec", "dom", None),
        P(),
        P("vec", None),
        P("dom", None),
        P("vec"),
        P("vec"),
    )
    out_specs = P("cuts", None, "vec", "dom", None)
    return jax.shard_map(
        functools.partial(local, torus), mesh=mesh, in_specs=in_specs, out_specs=out_specs, check_vma=False
    )
```

time: 503 us -> 154 us (0.31)
  the two profiles are of different devices: /device:TPU:4 before, /device:TPU:5 now
where the time goes in v1:
time: 154 us; the launch traced here: 153 us
  Pallas kernels  142 us (92%)
  other arithmetic  10.5 us (7%)
    pallas_call x1, Pallas kernels, call(): pl.pallas_call(functools.partial(kernel, ny, nz), out_shape=(jax.ShapeDty...  142 us
    broadcast_in_dim x1, other arithmetic, local(): return jnp.where(is_leader, fine_end, fine_end + change.astype(F32))[None]  10.5 us

profile of v1, /device:TPU:5, one launch (start us, length us, event | category | flops | bytes accessed | tf_op | source)
XLA Modules:
  0.0 153.4 jit_solution(3512807461205746038)
XLA Ops:
  0.0 1.3 broadcast_in_dim.4.tail_ref
  1.3 141.5 %parareal.1 = (f32[2,16,96,768]{3,2,1,0:T(8,128)}, bf16[2,16,96,768]{3,2,1,0:T(8,128)(2,1)}) custom-call(bf16[2,16,96,768]{3,2,1,0:T(8,128)(2,1)} %bitcast.3, bf16[768,768]{1,0:T(8,128)(2,1)} %y_hbm.1, bf16[768,1536]{1,0:T(8,128)(2,1)} %g_hbm.1, f32[96,768]{1,0:T(8,128)} %speed_hbm.1, bf16[96,96]{1,0:T(8,128)(2,1)} %constant.12.clone.a_ref, ...), custom_call_target="tpu_custom_call" | custom-call | tf_op jit(solution)/shard_map/parareal/pallas_call | solution.py:449
  142.8 10.5 %fusion = f32[1,2,16,96,768]{4,3,2,1,0:T(8,128)} fusion(f32[2,16,96,768]{3,2,1,0:T(8,128)} %get-tuple-element.7, bf16[2,16,96,768]{3,2,1,0:T(8,128)(2,1)} %get-tuple-element.8, pred[]{:T(512)S(6)} %eq.3), kind=kLoop, calls=%fused_computation.1 | loop fusion | flops 7077888 | bytes 23592960 | tf_op jit(solution)/shard_map/broadcast_in_dim | solution.py:501

commit v2 on v1

--- a/solution.py
+++ b/solution.py
@@ -15,7 +15,8 @@
 
 fine_step = 0.25
 penalty = 2.0
-lanes = 256
+lanes = 128
+block = 256
 pair = 2
 
 
@@ -48,11 +49,11 @@
 
 def kernel(
     ny, nz, s_hbm, y_hbm, g_hbm, speed_hbm, a_ref, tail_ref, damp_ref, coup_ref,
-    f_hbm, c_hbm,
-    s_own, s_next, tails, yop, speed, fine, mid, midb, ax, ay, halo_f, halo_b, halo_in, inflow,
-    dsend, lines, cbuf, gmat,
+    fine,
+    s_own, s_next, tails, yop, speed, mid, midb, ax, ay, halo_f, halo_b, halo_in, inflow,
+    dsend, lines, cbuf, gmat, c_in,
     in_sem, misc_sem, next_send, next_recv, g_send, g_recv, g_local, halo_send, halo_recv,
-    line_send, line_recv, x_send, c_send, c_recv, c_local, f_sem,
+    line_send, line_recv, x_send, c_send, c_recv,
 ):
     k = lax.axis_index("cuts")
     j = lax.axis_index("dom")
@@ -64,6 +65,7 @@
     _, waves, cols, ysize = s_hbm.shape
     chunks = ysize // lanes
     half = g_hbm.shape[0]
+    ahead = chunks // 2
     quarter = half // 4
 
     def order(t):
@@ -75,6 +77,25 @@
         return pltpu.make_async_remote_copy(
             src_ref=src, dst_ref=dst, send_sem=send, recv_sem=recv, device_id=at, device_id_type=MESH
         )
+
+    twin = (k + 1 - 2 * core, j, v)
+    barrier = pltpu.get_barrier_semaphore()
+
+    def greet(at):
+        pl.semaphore_signal(barrier, inc=1, device_id=at, device_id_type=MESH)
+
+    def greet_dom(t, carry):
+        at = lax.rem(j + t, dom)
+        greet((k, at, v))
+        greet((k + 1 - 2 * core, at, v))
+        return carry
+
+    lax.fori_loop(1, dom, greet_dom, 0)
+    greet(twin)
+    for there in (k, twin[0]):
+        greet((lax.rem(there + 2, 4), j, v))
+    greet((k, j, 1 - v))
+    greet((lax.rem(k + 2, 4), j, 1 - v))
 
     load_tails = pltpu.make_async_copy(s_hbm.at[:, :, pl.ds(cols - NP, NP), :], tails, misc_sem.at[0])
     load_y = pltpu.make_async_copy(y_hbm, yop, misc_sem.at[1])
@@ -92,42 +113,28 @@
 
     lax.fori_loop(0, waves, start_wave, 0)
 
+    half_rows = half // 2
     own_at = pl.multiple_of(v * half, half)
     other_at = pl.multiple_of((1 - v) * half, half)
     load_g = pltpu.make_async_copy(g_hbm, gmat.at[pl.ds(own_at, half)], g_local)
     load_g.start()
 
-    def send_g(side):
-        rows = pl.multiple_of((2 * side + core) * quarter, quarter)
-        at = (k if side == 0 else lax.rem(k + 2, 4), j, 1 - v)
+    def send_g(to, queue):
+        rows = pl.multiple_of(core * half_rows, half_rows)
         return remote(
-            g_hbm.at[pl.ds(rows, quarter)],
-            gmat.at[pl.ds(pl.multiple_of(own_at + rows, quarter), quarter)],
-            g_send.at[side], g_recv.at[side], at,
+            g_hbm.at[pl.ds(rows, half_rows)],
+            gmat.at[pl.ds(pl.multiple_of(own_at + rows, half_rows), half_rows)],
+            g_send.at[queue], g_recv.at[0], (to, j, 1 - v),
         )
 
-    def pass_g(side):
-        rows = pl.multiple_of(other_at + (2 * side + core) * quarter, quarter)
-        part = gmat.at[pl.ds(rows, quarter)]
-        return remote(part, part, g_send.at[2 + side], g_recv.at[2 + side], (k + 1 - 2 * core, j, v))
-
-    send_g(0).start()
-    send_g(1).start()
+    def g_twin():
+        part = gmat.at[pl.ds(pl.multiple_of(other_at + core * half_rows, half_rows), half_rows)]
+        return remote(part, part, g_send.at[2], g_recv.at[1], twin)
 
     def send_next(i, w, at):
         return remote(
             s_hbm.at[:, w, :, pl.ds(i * lanes, lanes)], s_next.at[i, w], next_send, next_recv.at[i, w], at
         )
-
-    @pl.when(k > 0)
-    def _():
-        for i in range(chunks):
-
-            def start_next(t, carry):
-                send_next(i, order(t), (k - 1, j, v)).start()
-                return carry
-
-            lax.fori_loop(0, waves, start_next, 0)
 
     load_tails.wait()
     load_y.wait()
@@ -167,9 +174,26 @@
     def send_halo():
         return remote(halo_b, halo_in, halo_send, halo_recv, (k, j + 1, v))
 
+    pl.semaphore_wait(barrier, 2 * dom - 1 + 4)
+
     @pl.when(j < dom - 1)
     def _():
         send_halo().start()
+
+    @pl.when(k > 0)
+    def _():
+        for i in range(chunks):
+
+            def start_next(t, carry):
+                send_next(i, order(t), (k - 1, j, v)).start()
+                return carry
+
+            lax.fori_loop(0, waves, start_next, 0)
+
+    @pl.when(low)
+    def _():
+        send_g(k, 0).start()
+        send_g(k + 2, 1).start()
 
     @pl.when(j > 0)
     def _():
@@ -184,8 +208,8 @@
 
     def slope_products(values):
         flat = jnp.concatenate([x.reshape(2 * cols, ysize) for x in values], axis=0)
-        for at in range(0, ysize, lanes):
-            ay[:, at : at + lanes] = jnp.dot(flat, yop[:, at : at + lanes], preferred_element_type=F32)
+        for at in range(0, ysize, block):
+            ay[:, at : at + block] = jnp.dot(flat, yop[:, at : at + block], preferred_element_type=F32)
         for q, x in enumerate(values):
             for p in range(2):
                 ax[q, p] = jnp.dot(a_ref[...], x[p], preferred_element_type=F32)
@@ -215,7 +239,7 @@
         def _():
             send_next(i, w, (k + 1, j, v)).wait_recv()
             for p in range(2):
-                gap = (fine[w, p, :, i * lanes : (i + 1) * lanes] - s_next[i, w, p].astype(F32)).astype(BF16)
+                gap = (fine[p, w, :, i * lanes : (i + 1) * lanes] - s_next[i, w, p].astype(F32)).astype(BF16)
                 target = lines.at[core, i, pl.ds(pl.multiple_of(j * cols, cols), cols)]
                 mine = (w == j) & (core == p)
 
@@ -231,9 +255,6 @@
                         (k - core + p, w, v),
                     ).start()
 
-    def store_fine(w):
-        return pltpu.make_async_copy(fine.at[w], f_hbm.at[:, w], f_sem)
-
     def fine_waves(t, carry):
         ws = [order(t * pair + q) for q in range(pair)]
         for w in ws:
@@ -253,7 +274,7 @@
         for q, w in enumerate(ws):
 
             def put_fine(p, r, value):
-                fine[w, p, r : r + NP, :] = value
+                fine[p, w, r : r + NP, :] = value
 
             combine(
                 q, w, 1,
@@ -261,11 +282,11 @@
                 lambda p, r: midb[q, p, r : r + NP, :].astype(F32),
                 put_fine,
             )
-            store_fine(w).start()
 
             @pl.when(k != 1)
             def _():
-                emit(0, w)
+                for i in range(ahead):
+                    emit(i, w)
 
         return carry
 
@@ -280,16 +301,18 @@
 
     @pl.when(k == 1)
     def _():
-        emit_chunk(0)
-
-    for side in range(2):
-        send_g(side).wait_recv()
-        pass_g(side).start()
-    for i in range(1, chunks):
-        emit_chunk(i)
+        for i in range(ahead):
+            emit_chunk(i)
+
+    @pl.when(k != 1)
+    def _():
+        for i in range(ahead, chunks):
+            emit_chunk(i)
+
+    send_g(k, 0).wait_recv()
+    g_twin().start()
     load_g.wait()
-    for side in range(2):
-        pass_g(side).wait_recv()
+    g_twin().wait_recv()
 
     gain = 1.0 / (1.0 + 2.0 * fine_step * jnp.full((1, lanes), damp_ref[j], F32))
     group = nz * cols
@@ -298,27 +321,24 @@
         part = lines.at[b, i, pl.ds(0, (dom - less) * cols)]
         remote(part, part, line_send.at[b], line_recv.at[b, i], (k, j, v)).wait_recv()
 
-    def piece_of(source, i, at, to, queue):
-        rows = pl.ds(pl.multiple_of(at * cols, cols), cols)
-        spot = c_hbm.at[core, j, :, pl.ds(i * lanes, lanes)]
-        return remote(source.at[rows], spot, c_send.at[queue], c_recv.at[core, i], (to, at, v))
-
-    def own_piece(source, i, at):
-        rows = pl.ds(pl.multiple_of(at * cols, cols), cols)
-        return pltpu.make_async_copy(source.at[rows], c_hbm.at[core, j, :, pl.ds(i * lanes, lanes)], c_local.at[i])
+    def spot(i, w, p):
+        return c_in.at[p, w, :, pl.ds(i * lanes, lanes)]
 
     def send_pieces(source, i, block, to, queue):
         def step(t, carry):
             at = block * nz + lax.rem(z + t, nz)
+            rows = pl.ds(pl.multiple_of(at * cols, cols), cols)
             mine = (at == j) & (k == to)
 
             @pl.when(mine)
             def _():
-                own_piece(source, i, at).start()
+                c_in[core, j, :, i * lanes : (i + 1) * lanes] = source[rows, :]
 
             @pl.when(jnp.logical_not(mine))
             def _():
-                piece_of(source, i, at, to, queue).start()
+                remote(
+                    source.at[rows], spot(i, j, core), c_send.at[queue], c_recv.at[core, i], (to, at, v)
+                ).start()
 
             return carry
 
@@ -346,30 +366,35 @@
     def across(i, rows):
         return remote(cbuf.at[1, i, rows], lines.at[1, i, rows], x_send, line_recv.at[1, i], (k + 2, j, v))
 
+    def wait_pieces(p, i, less):
+        part = cbuf.at[0, 0, pl.ds(0, (dom - less) * cols)]
+        remote(part, part, c_send.at[0], c_recv.at[p, i], (k, j, v)).wait_recv()
+
+    def wait_both(b, i):
+        @pl.when(core == b)
+        def _():
+            wait_lines(b, i, 1)
+
+        @pl.when(core != b)
+        def _():
+            wait_lines(b, i, 0)
+
     for i in range(chunks):
-
-        @pl.when(core == 0)
-        def _():
-            wait_lines(0, i, 1)
-
-        @pl.when(core == 1)
-        def _():
-            wait_lines(0, i, 0)
+        wait_both(0, i)
 
         @pl.when(low)
         def _():
-            product(lines.at[0, i], cbuf.at[0, i], lambda block, rows: send_pieces(cbuf.at[0, i], i, block, 1, 0))
-
-            @pl.when(core == 0)
-            def _():
-                wait_lines(1, i, 0)
-
-            @pl.when(core == 1)
-            def _():
-                wait_lines(1, i, 1)
-
+            product(lines.at[0, i], cbuf.at[0, i], lambda block, rows: None)
+
+            wait_both(1, i)
             add_lines(lines.at[1, i], cbuf.at[0, i])
             product(lines.at[1, i], cbuf.at[1, i], lambda block, rows: across(i, rows).start())
+
+            if i + ahead < chunks:
+
+                @pl.when(k == 1)
+                def _():
+                    emit_chunk(i + ahead)
 
         @pl.when(jnp.logical_not(low))
         def _():
@@ -383,26 +408,48 @@
             add_lines(lines.at[0, i], lines.at[1, i])
             product(lines.at[0, i], cbuf.at[0, i], lambda block, rows: send_pieces(cbuf.at[0, i], i, block, 3, 0))
 
+    @pl.when(low)
+    def _():
+        for i in range(chunks):
+
+            def give(t, carry):
+                send_pieces(cbuf.at[0, i], i, lax.rem(y + t, ny), 1, 0)
+                return carry
+
+            lax.fori_loop(0, ny, give, 0)
+
+    @pl.when(k > 0)
+    def _():
+        for i in range(chunks):
+            for p in range(2):
+
+                @pl.when(core == p)
+                def _():
+                    wait_pieces(p, i, 1)
+
+                @pl.when(core != p)
+                def _():
+                    wait_pieces(p, i, 0)
+
+            at = slice(i * lanes, (i + 1) * lanes)
+
+            def add_change(w, carry):
+                for p in range(2):
+                    fine[p, w, :, at] = fine[p, w, :, at] + c_in[p, w, :, at].astype(F32)
+                return carry
+
+            lax.fori_loop(0, waves, add_change, 0)
+
     def done(part, send, recv):
         return remote(part, part, send, recv, (k, j, v))
 
     def block_of(less):
         return cbuf.at[0, :, pl.ds(0, (dom - less) * cols)]
 
-    def line_of(less):
-        return cbuf.at[0, 0, pl.ds(0, (dom - less) * cols)]
-
     for p in range(2):
 
         @pl.when(core == p)
         def _():
-            @pl.when(k > 0)
-            def _():
-                for i in range(chunks):
-                    done(line_of(1), c_send.at[0], c_recv.at[p, i]).wait_recv()
-                    done(line_of(0), c_send.at[0], c_recv.at[1 - p, i]).wait_recv()
-                    own_piece(cbuf.at[0, i], i, 0).wait()
-
             @pl.when(k < 3)
             def _():
                 done(block_of(1), line_send.at[p], c_recv.at[0, 0]).wait_send()
@@ -426,10 +473,12 @@
     def _():
         send_halo().wait_send()
 
-    for side in range(2):
-        send_g(side).wait_send()
-        pass_g(side).wait_send()
-    pltpu.make_async_copy(f_hbm, f_hbm, f_sem).wait()
+    @pl.when(low)
+    def _():
+        send_g(k, 0).wait_send()
+        send_g(k + 2, 1).wait_send()
+
+    g_twin().wait_send()
 
 
 def call(torus, state, y_operator, coarse_inverse, base_speed, damping, coupling):
@@ -441,26 +490,22 @@
     length = dom * cols
     table = advect_matrix(cols)
     a_mat = jnp.asarray(table, BF16)
-    tail = jnp.broadcast_to(jnp.asarray(table[-1, -NP:], F32)[:, None], (NP, 128))
+    tail = jnp.asarray(np.repeat(table[-1, -NP:, None], 128, axis=1), F32)
     anywhere = pl.BlockSpec(memory_space=pl.ANY)
     vmem = pl.BlockSpec(memory_space=pltpu.VMEM)
     smem = pl.BlockSpec(memory_space=pltpu.SMEM)
     dma = pltpu.SemaphoreType.DMA
     return pl.pallas_call(
         functools.partial(kernel, ny, nz),
-        out_shape=(
-            jax.ShapeDtypeStruct(state.shape, F32),
-            jax.ShapeDtypeStruct(state.shape, BF16),
-        ),
+        out_shape=pltpu.VMEM(state.shape, F32),
         in_specs=[anywhere] * 4 + [vmem] * 2 + [smem] * 2,
-        out_specs=(anywhere, anywhere),
+        out_specs=vmem,
         scratch_shapes=[
             pltpu.VMEM((waves, 2, cols, ysize), BF16),
             pltpu.VMEM((chunks, waves, 2, cols, lanes), BF16),
             pltpu.VMEM((2, waves, NP, ysize), BF16),
             pltpu.VMEM((ysize, ysize), BF16),
             pltpu.VMEM((cols, ysize), F32),
-            pltpu.VMEM((waves, 2, cols, ysize), F32),
             pltpu.VMEM((pair, 2, cols, ysize), F32),
             pltpu.VMEM((pair, 2, cols, ysize), BF16),
             pltpu.VMEM((pair, 2, cols, ysize), F32),
@@ -473,12 +518,13 @@
             pltpu.VMEM((2, chunks, length, lanes), BF16),
             pltpu.VMEM((2, chunks, length, lanes), BF16),
             pltpu.VMEM((length, length), BF16),
+            pltpu.VMEM((2, waves, cols, ysize), BF16),
             dma((waves,)),
             dma((3,)),
             dma,
             dma((chunks, waves)),
-            dma((4,)),
-            dma((4,)),
+            dma((3,)),
+            dma((2,)),
             dma,
             dma,
             dma,
@@ -487,18 +533,14 @@
             dma,
             dma((2,)),
             dma((2, chunks)),
-            dma((chunks,)),
-            dma,
         ],
-        compiler_params=pltpu.CompilerParams(has_side_effects=True, vmem_limit_bytes=62 * 2**20),
+        compiler_params=pltpu.CompilerParams(collective_id=0, has_side_effects=True, vmem_limit_bytes=50 * 2**20),
         name="parareal",
     )(state, y_operator, coarse_inverse, base_speed, a_mat, tail, damping, coupling)
 
 
 def local(torus, starts_old, y_operator, coarse_inverse, base_speed, damping, coupling):
-    fine_end, change = call(torus, starts_old[0], y_operator, coarse_inverse, base_speed, damping, coupling)
-    is_leader = lax.axis_index("cuts") == 0
-    return jnp.where(is_leader, fine_end, fine_end + change.astype(F32))[None]
+    return call(torus, starts_old[0], y_operator, coarse_inverse, base_speed, damping, coupling)[None]
 
 
 def solution(mesh):

time: 154 us -> 113 us (0.73)
  Pallas kernels: 142 us -> 108 us
  other arithmetic: 10.5 us -> 0 us
  local copies, waits for them, and re-layouts: 1.32 us -> 3.74 us
    pallas_call x1, Pallas kernels: 142 us -> 108 us  [call(): pl.pallas_call(functools.partial(kernel, ny, nz), out_shape=pltpu.VMEM(st...]
    broadcast_in_dim x1 -> x0, other arithmetic: 10.5 us -> none  [local(): return jnp.where(is_leader, fine_end, fine_end + change.astype(F32))[None]]
    unnamed x0 -> x1, local copies, waits for them, and re-layouts: none -> 3.74 us
where the time goes in v2:
time: 113 us; the launch traced here: 112 us
  Pallas kernels  108 us (96%)
  local copies, waits for them, and re-layouts  3.74 us (3%)
    pallas_call x1, Pallas kernels, call(): pl.pallas_call(functools.partial(kernel, ny, nz), out_shape=pltpu.VMEM(st...  108 us
    unnamed x1, local copies, waits for them, and re-layouts  3.74 us

profile of v2, /device:TPU:5, one launch (start us, length us, event | category | flops | bytes accessed | tf_op | source)
XLA Modules:
  0.0 112.2 jit_solution(16600801723826701332)
XLA Ops:
  0.0 108.4 %parareal.1 = f32[2,16,96,768]{3,2,1,0:T(8,128)S(1)} custom-call(bf16[2,16,96,768]{3,2,1,0:T(8,128)(2,1)} %bitcast.3, bf16[768,768]{1,0:T(8,128)(2,1)} %y_hbm.1, bf16[768,1536]{1,0:T(8,128)(2,1)} %g_hbm.1, f32[96,768]{1,0:T(8,128)} %speed_hbm.1, bf16[96,96]{1,0:T(8,128)(2,1)} %constant.4.clone.a_ref, f32[16,128]{1,0:T(8,128)} %constant.5.clone.tail_ref, ...), custom_call_target="tpu_custom_call" | custom-call | tf_op jit(solution)/shard_map/parareal/pallas_call | solution.py:498
  108.5 3.7 %copy.10 = f32[1,2,16,96,768]{4,3,2,1,0:T(8,128)} copy(f32[1,2,16,96,768]{4,3,2,1,0:T(8,128)S(1)} %bitcast.2) | data formatting | bytes 18874368

commit v3 on v2

--- a/solution.py
+++ b/solution.py
@@ -53,7 +53,7 @@
     s_own, s_next, tails, yop, speed, mid, midb, ax, ay, halo_f, halo_b, halo_in, inflow,
     dsend, lines, cbuf, gmat, c_in,
     in_sem, misc_sem, next_send, next_recv, g_send, g_recv, g_local, halo_send, halo_recv,
-    line_send, line_recv, x_send, c_send, c_recv,
+    line_send, line_recv, x_send, x_recv, c_send, c_recv,
 ):
     k = lax.axis_index("cuts")
     j = lax.axis_index("dom")
@@ -304,7 +304,7 @@
         for i in range(ahead):
             emit_chunk(i)
 
-    @pl.when(k != 1)
+    @pl.when(k == 2)
     def _():
         for i in range(ahead, chunks):
             emit_chunk(i)
@@ -363,8 +363,16 @@
 
         lax.fori_loop(0, dom, step, 0)
 
-    def across(i, rows):
-        return remote(cbuf.at[1, i, rows], lines.at[1, i, rows], x_send, line_recv.at[1, i], (k + 2, j, v))
+    def across(i, block, to):
+        rows = pl.ds(pl.multiple_of(block * group, group), group)
+        return remote(cbuf.at[1, i, rows], lines.at[1, i, rows], x_send, x_recv.at[i * ny + block], (to, j, v))
+
+    def give(i):
+        def step(t, carry):
+            send_pieces(cbuf.at[0, i], i, lax.rem(y + t, ny), 1, 0)
+            return carry
+
+        lax.fori_loop(0, ny, step, 0)
 
     def wait_pieces(p, i, less):
         part = cbuf.at[0, 0, pl.ds(0, (dom - less) * cols)]
@@ -388,20 +396,21 @@
 
             wait_both(1, i)
             add_lines(lines.at[1, i], cbuf.at[0, i])
-            product(lines.at[1, i], cbuf.at[1, i], lambda block, rows: across(i, rows).start())
+            product(lines.at[1, i], cbuf.at[1, i], lambda block, rows: across(i, block, k + 2).start())
 
             if i + ahead < chunks:
-
-                @pl.when(k == 1)
-                def _():
-                    emit_chunk(i + ahead)
+                emit_chunk(i + ahead)
+
+            if i >= 3:
+                give(i - 3)
 
         @pl.when(jnp.logical_not(low))
         def _():
-            wait_lines(1, i, 0)
 
             def forward(t, carry):
-                send_pieces(lines.at[1, i], i, lax.rem(y + t, ny), 2, 1)
+                block = lax.rem(y + t, ny)
+                across(i, block, k - 2).wait_recv()
+                send_pieces(lines.at[1, i], i, block, 2, 1)
                 return carry
 
             lax.fori_loop(0, ny, forward, 0)
@@ -410,13 +419,8 @@
 
     @pl.when(low)
     def _():
-        for i in range(chunks):
-
-            def give(t, carry):
-                send_pieces(cbuf.at[0, i], i, lax.rem(y + t, ny), 1, 0)
-                return carry
-
-            lax.fori_loop(0, ny, give, 0)
+        for i in range(chunks - 3, chunks):
+            give(i)
 
     @pl.when(k > 0)
     def _():
@@ -531,6 +535,7 @@
             dma((2,)),
             dma((2, chunks)),
             dma,
+            dma((chunks * ny,)),
             dma((2,)),
             dma((2, chunks)),
         ],

time: 113 us -> 110 us (0.973)
  Pallas kernels: 108 us -> 106 us
    pallas_call x1, Pallas kernels: 108 us -> 106 us  [call(): pl.pallas_call(functools.partial(kernel, ny, nz), out_shape=pltpu.VMEM(st...]
where the time goes in v3:
time: 110 us
  Pallas kernels  106 us (96%)
  local copies, waits for them, and re-layouts  3.74 us (3%)
    pallas_call x1, Pallas kernels, call(): pl.pallas_call(functools.partial(kernel, ny, nz), out_shape=pltpu.VMEM(st...  106 us
    unnamed x1, local copies, waits for them, and re-layouts  3.74 us

profile of v3, /device:TPU:5, one launch (start us, length us, event | category | flops | bytes accessed | tf_op | source)
XLA Modules:
  0.0 109.6 jit_solution(14324692190918160230)
XLA Ops:
  0.0 105.8 %parareal.1 = f32[2,16,96,768]{3,2,1,0:T(8,128)S(1)} custom-call(bf16[2,16,96,768]{3,2,1,0:T(8,128)(2,1)} %bitcast.3, bf16[768,768]{1,0:T(8,128)(2,1)} %y_hbm.1, bf16[768,1536]{1,0:T(8,128)(2,1)} %g_hbm.1, f32[96,768]{1,0:T(8,128)} %speed_hbm.1, bf16[96,96]{1,0:T(8,128)(2,1)} %constant.4.clone.a_ref, f32[16,128]{1,0:T(8,128)} %constant.5.clone.tail_ref, ...), custom_call_target="tpu_custom_call" | custom-call | tf_op jit(solution)/shard_map/parareal/pallas_call | solution.py:502
  105.8 3.7 %copy.10 = f32[1,2,16,96,768]{4,3,2,1,0:T(8,128)} copy(f32[1,2,16,96,768]{4,3,2,1,0:T(8,128)S(1)} %bitcast.2) | data formatting | bytes 18874368

commit v4 on v3

--- a/solution.py
+++ b/solution.py
@@ -136,6 +136,23 @@
             s_hbm.at[:, w, :, pl.ds(i * lanes, lanes)], s_next.at[i, w], next_send, next_recv.at[i, w], at
         )
 
+    pl.semaphore_wait(barrier, 2 * dom - 1 + 4)
+
+    @pl.when(k > 0)
+    def _():
+        for i in range(chunks):
+
+            def start_next(t, carry):
+                send_next(i, order(t), (k - 1, j, v)).start()
+                return carry
+
+            lax.fori_loop(0, waves, start_next, 0)
+
+    @pl.when(low)
+    def _():
+        send_g(k, 0).start()
+        send_g(k + 2, 1).start()
+
     load_tails.wait()
     load_y.wait()
     load_speed.wait()
@@ -174,26 +191,9 @@
     def send_halo():
         return remote(halo_b, halo_in, halo_send, halo_recv, (k, j + 1, v))
 
-    pl.semaphore_wait(barrier, 2 * dom - 1 + 4)
-
     @pl.when(j < dom - 1)
     def _():
         send_halo().start()
-
-    @pl.when(k > 0)
-    def _():
-        for i in range(chunks):
-
-            def start_next(t, carry):
-                send_next(i, order(t), (k - 1, j, v)).start()
-                return carry
-
-            lax.fori_loop(0, waves, start_next, 0)
-
-    @pl.when(low)
-    def _():
-        send_g(k, 0).start()
-        send_g(k + 2, 1).start()
 
     @pl.when(j > 0)
     def _():

time: 110 us -> 109 us (level)
    pallas_call x1, Pallas kernels: 106 us -> 105 us  [call(): pl.pallas_call(functools.partial(kernel, ny, nz), out_shape=pltpu.VMEM(st...]
where the time goes in v4:
time: 109 us; the launch traced here: 108 us
  Pallas kernels  105 us (96%)
  local copies, waits for them, and re-layouts  3.74 us (3%)
    pallas_call x1, Pallas kernels, call(): pl.pallas_call(functools.partial(kernel, ny, nz), out_shape=pltpu.VMEM(st...  105 us
    unnamed x1, local copies, waits for them, and re-layouts  3.74 us

profile of v4, /device:TPU:5, one launch (start us, length us, event | category | flops | bytes accessed | tf_op | source)
XLA Modules:
  0.0 108.4 jit_solution(3646347355214609119)
XLA Ops:
  0.0 104.7 %parareal.1 = f32[2,16,96,768]{3,2,1,0:T(8,128)S(1)} custom-call(bf16[2,16,96,768]{3,2,1,0:T(8,128)(2,1)} %bitcast.3, bf16[768,768]{1,0:T(8,128)(2,1)} %y_hbm.1, bf16[768,1536]{1,0:T(8,128)(2,1)} %g_hbm.1, f32[96,768]{1,0:T(8,128)} %speed_hbm.1, bf16[96,96]{1,0:T(8,128)(2,1)} %constant.4.clone.a_ref, f32[16,128]{1,0:T(8,128)} %constant.5.clone.tail_ref, ...), custom_call_target="tpu_custom_call" | custom-call | tf_op jit(solution)/shard_map/parareal/pallas_call | solution.py:502
  104.7 3.7 %copy.10 = f32[1,2,16,96,768]{4,3,2,1,0:T(8,128)} copy(f32[1,2,16,96,768]{4,3,2,1,0:T(8,128)S(1)} %bitcast.2) | data formatting | bytes 18874368
